TPU v7x, 32 devices: a whole 2x2x4 slice. The times are simulated.
32 devices in a mesh: dp: 4 (over y, core), expert: 4 (over z), tensor: 2 (over x).
Axes of the slice: x: 2, y: 2, z: 4, core: 2. Of those that a mesh axis runs over, the one named last changes fastest.
Arguments:
- tokens: bfloat16 [96, 7168], P('expert', 'tensor'), may hold values from -6 to 6
- expert_ids: int32 [96, 8], P('expert'), may hold values from 0 to 63, all different within a row; in each aligned block of 24 rows (0 to 23, 24 to 47, ...) at most 4 rows name the same one
- gate_weights: float32 [96, 8], P('expert'), may hold values from 0.1 to 1
- w_gate: bfloat16 [64, 7168, 1024], P('expert', 'tensor', 'dp'), may hold values from -0.0625 to 0.0625
- w_up: bfloat16 [64, 7168, 1024], P('expert', 'tensor', 'dp'), may hold values from -0.0625 to 0.0625
- w_down: bfloat16 [64, 1024, 7168], P('expert', 'dp', 'tensor'), may hold values from -0.1875 to 0.1875
Outputs:
- mixed: bfloat16 [96, 7168], P('expert', 'tensor')
Inputs may be any that keep to these rules, and one draw needn't show every extreme that they name: `expert_ids`: each row names 8 different experts. Among the rows of one index of the expert axis (aligned blocks of 24 rows) no expert is named more than 4 times, and in some block one expert is named exactly 4 times.
All inputs are finite; a program needn't handle non-finite values.
Results may differ from a plain program's by a relative error of at most 0.0049.
Values may be sent and summed in bfloat16 or wider, within the bound.
No kernel may reach another device: no remote copies, remote signals or barrier semaphores. Data moves between devices by JAX's collectives and lax.ppermute only.
A program may use at most 128 MiB of HBM per device.

v0:
```python
import jax
import jax.numpy as jnp
from jax import lax
from jax.sharding import PartitionSpec as P

TOP = 8
CAP = 4


def per_device(tokens, expert_ids, gate_weights, w_gate, w_up, w_down):
    expert_count = lax.axis_size("expert")
    hidden_count = lax.axis_size("dp")
    local_experts = w_gate.shape[0]
    tok_rows = tokens.shape[0]
    feature_cols = tokens.shape[1]
    total_experts = local_experts * expert_count
    cap_share = CAP // hidden_count
    slot_total = local_experts * CAP * expert_count
    flat_ids = expert_ids.reshape(-1)
    one_hot = (flat_ids[:, None] == lax.iota(jnp.int32, total_experts)[None, :]).astype(jnp.int32)
    earlier = jnp.cumsum(one_hot, axis=0) - one_hot
    slot_rank = jnp.sum(earlier * one_hot, axis=1)
    owner_device = flat_ids // local_experts
    within = flat_ids % local_experts
    send_slot = (within * CAP + slot_rank) * expert_count + owner_device
    dispatch_table = (send_slot[None, :] == lax.iota(jnp.int32, slot_total)[:, None]).astype(
        jnp.float32
    )
    dispatch_table = jnp.sum(dispatch_table.reshape(slot_total, tok_rows, TOP), axis=2).astype(
        jnp.bfloat16
    )
    outbound = jnp.dot(dispatch_table, tokens, preferred_element_type=jnp.float32).astype(
        jnp.bfloat16
    )
    outbound = outbound.reshape(local_experts, CAP, expert_count, feature_cols)
    arrived = lax.all_to_all(outbound, "expert", split_axis=2, concat_axis=2, tiled=True)
    expert_rows = arrived.reshape(local_experts, CAP * expert_count, feature_cols)
    gate_part = jnp.einsum("lrd,ldf->lrf", expert_rows, w_gate, preferred_element_type=jnp.float32)
    up_part = jnp.einsum("lrd,ldf->lrf", expert_rows, w_up, preferred_element_type=jnp.float32)
    gate_sum, up_sum = (
        lax.psum_scatter(gate_part, "tensor", scatter_dimension=1, tiled=True),
        lax.psum_scatter(up_part, "tensor", scatter_dimension=1, tiled=True),
    )
    hidden_share = (jax.nn.silu(gate_sum) * up_sum).astype(jnp.bfloat16)
    hidden = lax.all_gather(hidden_share, "tensor", axis=1, tiled=True)
    partial_value = jnp.einsum("lrf,lfd->lrd", hidden, w_down, preferred_element_type=jnp.float32)
    outputs = lax.psum_scatter(partial_value, "dp", scatter_dimension=1, tiled=True)
    backward = outputs.reshape(local_experts, cap_share, expert_count, feature_cols)
    returned = lax.all_to_all(backward, "expert", split_axis=2, concat_axis=2, tiled=True)
    table_cols = local_experts * cap_share * expert_count
    returned = returned.reshape(table_cols, feature_cols)
    block_index = lax.axis_index("dp")
    is_mine = (slot_rank // cap_share == block_index).astype(jnp.float32)
    position = (within * cap_share + slot_rank % cap_share) * expert_count + owner_device
    scaled = gate_weights.reshape(-1) * is_mine
    combine_table = jnp.where(
        position[:, None] == lax.iota(jnp.int32, table_cols)[None, :], scaled[:, None], 0.0
    )
    combine_table = jnp.sum(combine_table.reshape(tok_rows, TOP, table_cols), axis=1)
    partial_mix = jnp.dot(
        combine_table, returned, precision=lax.Precision.HIGHEST, preferred_element_type=jnp.float32
    )
    mixed = lax.psum(partial_mix, "dp")
    return mixed.astype(jnp.bfloat16)


def solution(mesh):
    in_specs = (
        P("expert", "tensor"),
        P("expert", None),
        P("expert", None),
        P("expert", "tensor", "dp"),
        P("expert", "tensor", "dp"),
        P("expert", "dp", "tensor"),
    )
    out_specs = P("expert", "tensor")
    return jax.shard_map(
        per_device, mesh=mesh, in_specs=in_specs, out_specs=out_specs, check_vma=False
    )
```

profile of v0, /device:TPU:0, one launch (start us, length us, event | category | flops | bytes accessed | tf_op | source)
XLA Modules:
  0.0 219.1 jit_solution(13099469717093298027)
XLA Ops:
  6.5 0.0 copy-start
  6.5 0.0 reduce-scatter.4.cloned.1.call-start
  6.5 0.8 copy.43
  7.3 0.1 eq.66
  7.5 0.6 reduce-window.6
  8.1 0.2 slice_reduce_fusion
  8.3 0.1 bitcast_bitcast_fusion
  8.4 0.1 reduce_sum.30
  8.6 0.1 convert_reduce_fusion
  8.7 0.0 copy-done
  8.7 1.9 convolution_convert_fusion
  10.6 3.1 %reshape.151 = bf16[16,4,4,3584]{3,2,1,0:T(4,128)(2,1)S(1)} reshape(bf16[256,3584]{1,0:T(8,128)(2,1)} %convolution_convert_fusion) | data formatting | bytes 3670016 | tf_op jit(solution)/shard_map/reshape | solution.py:35
  13.8 0.7 copy.51
  14.5 48.7 %all_to_all.10 = bf16[16,4,4,3584]{3,1,0,2:T(4,128)(2,1)S(1)} all-to-all(bf16[16,4,4,3584]{3,1,0,2:T(4,128)(2,1)S(1)} %copy.51), channel_id=1, replica_groups=mesh['dp'=4,'expert'=4,'tensor'=2] {'expert'}, dimensions={2} | all-to-all | bytes 3670016 | tf_op jit(solution)/shard_map/all_to_all | solution.py:36
  63.2 2.7 %copy.52 = bf16[16,4,4,3584]{3,2,1,0:T(4,128)(2,1)} copy(bf16[16,4,4,3584]{3,1,0,2:T(4,128)(2,1)S(1)} %all_to_all.10) | data formatting | bytes 3670016 | tf_op jit(solution)/shard_map/all_to_all | solution.py:36
  65.9 2.9 %reshape.152 = bf16[16,16,3584]{2,1,0:T(8,128)(2,1)S(1)} reshape(bf16[16,4,4,3584]{3,2,1,0:T(4,128)(2,1)} %copy.52) | data formatting | bytes 3670016 | tf_op jit(solution)/shard_map/reshape | solution.py:37
  68.8 12.1 %fusion.7 = f32[16,16,256]{2,1,0:T(8,128)} fusion(bf16[16,16,3584]{2,1,0:T(8,128)(2,1)S(1)} %reshape.152, bf16[16,3584,256]{2,1,0:T(8,128)(2,1)} %param.9), kind=kOutput, calls=%fused_computation.29 | convolution fusion | flops 469762048 | bytes 31457280 | tf_op jit(solution)/shard_map/lrd,ldf->lrf/dot_general | solution.py:38
  80.9 0.0 reduce-scatter.4.cloned.1.call-update
  80.9 0.0 reduce-scatter.6.cloned.1.call-start
  81.0 12.2 %fusion.8 = f32[16,16,256]{2,1,0:T(8,128)} fusion(bf16[16,16,3584]{2,1,0:T(8,128)(2,1)S(1)} %reshape.152, bf16[16,3584,256]{2,1,0:T(8,128)(2,1)} %param.10), kind=kOutput, calls=%fused_computation.30 | convolution fusion | flops 469762048 | bytes 31457280 | tf_op jit(solution)/shard_map/lrd,ldf->lrf/dot_general | solution.py:39
  93.1 0.0 reduce-scatter.6.cloned.1.call-update
  93.2 0.0 reduce-scatter.8.cloned.1.call-start
  93.2 0.0 reduce-scatter.4.cloned.1.call-done
  93.2 12.8 %reduce-scatter.6.cloned.1.call-done = f32[16,8,256]{2,1,0:T(8,128)} async-done(((f32[16,16,256]{2,1,0:T(8,128)}), f32[16,8,256]{2,1,0:T(8,128)}) %reduce-scatter.6.cloned.1.call-update) | async-done | bytes 131088 | tf_op jit(solution)/shard_map/reduce_scatter | solution.py:42
  106.0 1.0 multiply_convert_fusion
  107.0 5.1 %all_gather.3 = bf16[16,16,256]{2,1,0:T(8,128)(2,1)S(1)} all-gather(bf16[16,8,256]{2,1,0:T(8,128)(2,1)S(1)} %multiply_convert_fusion), channel_id=1, replica_groups=mesh['dp'=4,'expert'=4,'tensor'=2] {'tensor'}, dimensions={1}, use_global_device_ids=true | all-gather | bytes 196608 | tf_op jit(solution)/shard_map/all_gather | solution.py:45
  112.2 11.4 %fusion.9 = f32[16,16,3584]{2,1,0:T(8,128)S(1)} fusion(bf16[16,16,256]{2,1,0:T(8,128)(2,1)S(1)} %all_gather.3, bf16[16,256,3584]{2,1,0:T(8,128)(2,1)} %param.11), kind=kOutput, calls=%fused_computation.31 | convolution fusion | flops 469762048 | bytes 33161216 | tf_op jit(solution)/shard_map/lrf,lfd->lrd/dot_general | solution.py:46
  123.5 3.9 %copy.53 = f32[16,16,3584]{2,0,1:T(8,128)} copy(f32[16,16,3584]{2,1,0:T(8,128)S(1)} %fusion.9) | data formatting | bytes 7340032 | tf_op jit(solution)/shard_map/lrf,lfd->lrd/dot_general | solution.py:46
  127.5 0.0 copy-start.2
  127.5 0.0 reduce-scatter.8.cloned.1.call-update
  127.5 41.4 %reduce-scatter.8.cloned.1.call-done = f32[16,4,3584]{2,0,1:T(8,128)} async-done(((f32[16,16,3584]{2,0,1:T(8,128)}), f32[16,4,3584]{2,0,1:T(8,128)}) %reduce-scatter.8.cloned.1.call-update) | async-done | bytes 917520 | tf_op jit(solution)/shard_map/reduce_scatter | solution.py:47
  168.9 0.0 copy-start.1
  168.9 4.7 %all-to-all-start.1 = ((f32[16,1,4,3584]{3,0,1,2:T(8,128)}), f32[16,1,4,3584]{3,0,1,2:T(8,128)S(1)}, u32[]{:S(2)}, u32[]{:S(2)}) async-start(f32[16,1,4,3584]{3,0,1,2:T(8,128)} %bitcast.27), calls=%async_computation.4 | async-start | bytes 1835008 | tf_op jit(solution)/shard_map/all_to_all | solution.py:49
  173.6 0.0 copy-done.2
  173.6 0.1 copy.50
  173.7 0.1 select_reduce_fusion
  173.9 22.5 %all-to-all-done.1 = f32[16,1,4,3584]{3,0,1,2:T(8,128)S(1)} async-done(((f32[16,1,4,3584]{3,0,1,2:T(8,128)}), f32[16,1,4,3584]{3,0,1,2:T(8,128)S(1)}, u32[]{:S(2)}, u32[]{:S(2)}) %all-to-all-start.1) | async-done | bytes 917536 | tf_op jit(solution)/shard_map/all_to_all | solution.py:49
  196.4 0.6 copy.55
  197.0 0.3 reshape.154
  197.3 0.6 fusion.10
  197.9 14.7 %all-reduce.2 = bf16[24,3584]{1,0:T(8,128)(2,1)} all-reduce(f32[24,3584]{1,0:T(8,128)S(1)} %fusion.10), channel_id=1, replica_groups=mesh['dp'=4,'expert'=4,'tensor'=2] {'dp'}, use_global_device_ids=true, to_apply=%region_8.9 | all-reduce | flops 86016 | bytes 516096 | tf_op jit(solution)/shard_map/psum | solution.py:63
  212.6 0.0 copy-done.1
  (7 shorter events, 0.1 us)
Async XLA Ops:
  6.5 2.2 copy-start
  6.5 86.7 %reduce-scatter.4.cloned.1.call-start = ((), (), s32[]{:S(2)}) async-start(), calls=%async_computation.5 | async-start | bytes 393216 | tf_op jit(solution)/shard_map/reduce_scatter | solution.py:41
  80.9 25.1 %reduce-scatter.6.cloned.1.call-start = ((), (), s32[]{:S(2)}) async-start(), calls=%async_computation.6 | async-start | bytes 393216 | tf_op jit(solution)/shard_map/reduce_scatter | solution.py:42
  93.2 75.8 %reduce-scatter.8.cloned.1.call-start = ((), (), s32[]{:S(2)}) async-start(), calls=%async_computation.7 | async-start | bytes 4587520 | tf_op jit(solution)/shard_map/reduce_scatter | solution.py:47
  127.5 46.2 %copy-start.2 = (f32[24,8]{0,1:T(8,128)S(1)}, f32[24,8]{0,1:T(8,128)}, u32[]{:S(2)}) copy-start(f32[24,8]{0,1:T(8,128)} %param.8) | copy-start | bytes 2308
  168.9 43.7 %copy-start.1 = (bf16[24,3584]{1,0:T(8,128)(2,1)S(1)}, bf16[24,3584]{1,0:T(8,128)(2,1)}, u32[]{:S(2)}) copy-start(bf16[24,3584]{1,0:T(8,128)(2,1)} %param.6) | copy-start | bytes 516100
  168.9 27.5 %all-to-all-start.1 = ((f32[16,1,4,3584]{3,0,1,2:T(8,128)}), f32[16,1,4,3584]{3,0,1,2:T(8,128)S(1)}, u32[]{:S(2)}, u32[]{:S(2)}) async-start(f32[16,1,4,3584]{3,0,1,2:T(8,128)} %bitcast.27), calls=%async_computation.4 | async-start | bytes 1835008 | tf_op jit(solution)/shard_map/all_to_all | solution.py:49
Sparse Core Ops, SparseCore 0:
  81.0 10.9 reduce-scatter.3
  94.2 11.7 reduce-scatter.5
  127.6 41.2 reduce-scatter.7
where the time goes:
time: 220 us; the launch traced here: 219 us
  waiting for transfers between devices  76.8 us (35%)
  blocking collectives  68.6 us (31%)
  matrix products  38.1 us (17%)
  local copies, waits for them, and re-layouts  15.5 us (7%)
  between operations  13.2 us (6%)
  starting transfers between devices  4.8 us (2%)
    all_to_all x1, blocking collectives, per_device(): lax.all_to_all(outbound, 'expert', split_axis=2, concat_axis=2, tiled=True)  48.7 us
    reduce_scatter x1, waiting for transfers between devices, per_device(): lax.psum_scatter(partial_value, 'dp', scatter_dimension=1, tiled=True)  41.4 us
    all_to_all x1, waiting for transfers between devices, per_device(): lax.all_to_all(backward, 'expert', split_axis=2, concat_axis=2, tiled=True)  22.5 us
    psum x1, blocking collectives, per_device(): mixed = lax.psum(partial_mix, 'dp')  14.7 us
    reduce_scatter x1, waiting for transfers between devices, per_device(): lax.psum_scatter(up_part, 'tensor', scatter_dimension=1, tiled=True)  12.8 us
    dot_general x1, matrix products, per_device(): jnp.einsum('lrd,ldf->lrf', expert_rows, w_up, preferred_element_type=jnp....  12.2 us
    dot_general x1, matrix products, per_device(): jnp.einsum('lrd,ldf->lrf', expert_rows, w_gate, preferred_element_type=jn...  12.1 us
    dot_general x1, matrix products, per_device(): jnp.einsum('lrf,lfd->lrd', hidden, w_down, preferred_element_type=jnp.flo...  11.4 us
  transfers between devices with their start and end apart: 4, of which 3 were waited for; matrix products, arithmetic and copies ran while one was open for 6% of the time, Pallas kernels for 0%

commit v1 on v0

v1 whole, which is shorter than its diff:
```python
import functools

import jax
import jax.numpy as jnp
from jax import lax
from jax.experimental import pallas as pl
from jax.experimental.pallas import tpu as pltpu
from jax.sharding import PartitionSpec as P

CAP = 4
DIRECT = 8
VMEM_BYTES = 40 * 1024 * 1024


def rotate(x, axis, shift):
    n = lax.axis_size(axis)
    return lax.ppermute(x, axis, [(i, (i + shift) % n) for i in range(n)])


def selection(code, slots):
    experts, toks = code.shape
    wide = jnp.broadcast_to(code[:, None, :], (experts, slots, toks))
    place = lax.broadcasted_iota(jnp.int32, (experts, slots, toks), 1)
    return (wide == place).reshape(experts * slots, toks)


def up_kernel(n_pieces, slots, *refs):
    codes, pieces = refs[:n_pieces], refs[n_pieces : 2 * n_pieces]
    wg_ref, wu_ref, own_ref, send_ref, rows_ref = refs[2 * n_pieces :]
    step = pl.program_id(0)
    width = rows_ref.shape[1]
    chunk = 512 if width % 512 == 0 else width

    @pl.when(step == 0)
    def _():
        picks = [selection(c[...], slots).astype(jnp.bfloat16) for c in codes]
        for at in range(0, width, chunk):
            total = None
            for pick, piece in zip(picks, pieces):
                part = jnp.dot(
                    pick, piece[:, at : at + chunk], preferred_element_type=jnp.float32
                )
                total = part if total is None else total + part
            rows_ref[:, at : at + chunk] = total.astype(jnp.bfloat16)

    lhs = rows_ref[pl.ds(pl.multiple_of(step * slots, slots), slots), :]
    gate = jnp.dot(lhs, wg_ref[0], preferred_element_type=jnp.float32)
    up = jnp.dot(lhs, wu_ref[0], preferred_element_type=jnp.float32)
    ff = gate.shape[1]
    own_ref[:, :ff] = gate
    own_ref[:, ff:] = up
    send_ref[:, :ff] = gate.astype(jnp.bfloat16)
    send_ref[:, ff:] = up.astype(jnp.bfloat16)


def up_call(codes, pieces, w_gate, w_up, first, slots):
    experts = codes[0].shape[0]
    width, ff = w_gate.shape[1], w_gate.shape[2]
    whole = lambda a: pl.BlockSpec(a.shape, lambda e: (0,) * a.ndim)
    weight = pl.BlockSpec((1, width, ff), lambda e: (e + first, 0, 0))
    out = pl.BlockSpec((slots, 2 * ff), lambda e: (e, 0))
    return pl.pallas_call(
        functools.partial(up_kernel, len(pieces), slots),
        grid=(experts,),
        in_specs=[whole(c) for c in codes] + [whole(p) for p in pieces] + [weight, weight],
        out_specs=[out, out],
        out_shape=[
            jax.ShapeDtypeStruct((experts * slots, 2 * ff), jnp.float32),
            jax.ShapeDtypeStruct((experts * slots, 2 * ff), jnp.bfloat16),
        ],
        scratch_shapes=[pltpu.VMEM((experts * slots, width), jnp.bfloat16)],
        compiler_params=pltpu.CompilerParams(
            dimension_semantics=("arbitrary",), vmem_limit_bytes=VMEM_BYTES
        ),
        cost_estimate=pl.CostEstimate(
            flops=200 * experts * width * ff, bytes_accessed=4 * experts * width * ff,
            transcendentals=0,
        ),
        name="gate_up",
    )(*codes, *pieces, w_gate, w_up)


def down_kernel(n_recv, n_out, slots, last, *refs):
    refs = list(refs)
    refs.pop(0)
    code_ref, mix_ref, own_ref = refs[:3]
    recvs = refs[3 : 3 + n_recv]
    rest = refs[3 + n_recv :]
    if last:
        wd_ref, acc_ref = rest[:2]
        outs = rest[2 : 2 + n_out]
    else:
        wd_ref = rest[0]
        outs = rest[1:2]
    hid_ref, pick_ref, scale_ref, y_ref = rest[-4:]
    step = pl.program_id(0)
    experts, ff = wd_ref.shape[0], wd_ref.shape[1]

    @pl.when(step == 0)
    def _():
        sums = own_ref[...]
        for r in recvs:
            sums = sums + r[...].astype(jnp.float32)
        gate, up = sums[:, :ff], sums[:, ff:]
        hid_ref[...] = (gate / (1.0 + jnp.exp(-gate)) * up).astype(jnp.bfloat16)
        toks = code_ref.shape[1]
        chosen = selection(code_ref[...], slots)
        mix = jnp.broadcast_to(mix_ref[...][:, None, :], (experts, slots, toks))
        mix = mix.reshape(experts * slots, toks)
        scale_ref[...] = jnp.sum(jnp.where(chosen, mix, 0.0), axis=1, keepdims=True)
        pick_ref[...] = chosen.astype(jnp.float32).T.astype(jnp.bfloat16)

    for e in range(experts):
        rows = slice(e * slots, (e + 1) * slots)
        y = jnp.dot(hid_ref[rows, :], wd_ref[e], preferred_element_type=jnp.float32)
        y_ref[rows, :] = y * scale_ref[rows, :]
    y = y_ref[...]
    high = y.astype(jnp.bfloat16)
    low = (y - high.astype(jnp.float32)).astype(jnp.bfloat16)
    pick = pick_ref[...]
    mixed = jnp.dot(pick, high, preferred_element_type=jnp.float32) + jnp.dot(
        pick, low, preferred_element_type=jnp.float32
    )
    if last:
        mixed = mixed + acc_ref[0]
        for k, out in enumerate(outs):

            @pl.when(step == k)
            def _():
                out[...] = mixed.astype(out.dtype)
    else:
        outs[0][0] = mixed


def down_call(code, mix, own, recvs, w_down, acc, first, slots, n_out, index):
    experts, toks = code.shape
    ff, width = w_down.shape[1], w_down.shape[2]
    cols = width // n_out
    last = acc is not None
    whole = lambda a: pl.BlockSpec(a.shape, lambda j, s: (0,) * a.ndim)
    if cols % 128 == 0:
        weight = pl.BlockSpec(
            (experts, ff, cols), lambda j, s: (first // experts, 0, (s[0] + j) % n_out)
        )
    else:
        w_down = w_down[first : first + experts].reshape(experts, ff, n_out, cols)
        w_down = jnp.moveaxis(w_down, 2, 0).reshape(n_out * experts, ff, cols)
        weight = pl.BlockSpec((experts, ff, cols), lambda j, s: ((s[0] + j) % n_out, 0, 0))
    acc_spec = pl.BlockSpec((1, toks, cols), lambda j, s: (j, 0, 0))
    in_specs = [whole(code), whole(mix), whole(own)] + [whole(r) for r in recvs] + [weight]
    args = [code, mix, own, *recvs, w_down]
    if last:
        in_specs.append(acc_spec)
        args.append(acc)
        out_specs = [pl.BlockSpec((toks, cols), lambda j, s: (0, 0)) for _ in range(n_out)]
        out_shape = [
            jax.ShapeDtypeStruct((toks, cols), jnp.bfloat16 if k else jnp.float32)
            for k in range(n_out)
        ]
    else:
        out_specs = acc_spec
        out_shape = jax.ShapeDtypeStruct((n_out, toks, cols), jnp.float32)
    return pl.pallas_call(
        functools.partial(down_kernel, len(recvs), n_out, slots, last),
        grid_spec=pltpu.PrefetchScalarGridSpec(
            num_scalar_prefetch=1,
            grid=(n_out,),
            in_specs=in_specs,
            out_specs=out_specs,
            scratch_shapes=[
                pltpu.VMEM((experts * slots, ff), jnp.bfloat16),
                pltpu.VMEM((toks, experts * slots), jnp.bfloat16),
                pltpu.VMEM((experts * slots, 1), jnp.float32),
                pltpu.VMEM((experts * slots, cols), jnp.float32),
            ],
        ),
        out_shape=out_shape,
        compiler_params=pltpu.CompilerParams(
            dimension_semantics=("arbitrary",), vmem_limit_bytes=VMEM_BYTES
        ),
        cost_estimate=pl.CostEstimate(
            flops=200 * experts * width * ff, bytes_accessed=2 * experts * width * ff,
            transcendentals=0,
        ),
        name="down_mix",
    )(index, *args)


def per_device(tokens, expert_ids, gate_weights, w_gate, w_up, w_down):
    n_exp = lax.axis_size("expert")
    n_dp = lax.axis_size("dp")
    n_ten = lax.axis_size("tensor")
    local = w_gate.shape[0]
    rows = tokens.shape[0]
    total = local * n_exp
    slots = CAP * n_exp
    direct = n_exp <= DIRECT

    hit = expert_ids[None, :, :] == lax.iota(jnp.int32, total)[:, None, None]
    weight = jnp.sum(jnp.where(hit, gate_weights[None], 0.0), axis=2)
    named = jnp.any(hit, axis=2)
    earlier = lax.iota(jnp.int32, rows)[:, None] < lax.iota(jnp.int32, rows)[None, :]
    rank = jnp.dot(
        named.astype(jnp.bfloat16), earlier.astype(jnp.bfloat16),
        preferred_element_type=jnp.float32,
    )
    table = jnp.stack([weight, jnp.where(named, rank, -1.0)])

    if direct:
        pieces = [tokens] + [rotate(tokens, "expert", j) for j in range(1, n_exp)]
        tables = [table] + [rotate(table, "expert", j) for j in range(1, n_exp)]
        tables = jnp.stack(tables, axis=2)
    else:
        pieces = [lax.all_gather(tokens, "expert", axis=0, tiled=True)]
        tables = lax.all_gather(table, "expert", axis=2)
    tables = lax.dynamic_slice_in_dim(tables, lax.axis_index("expert") * local, local, axis=1)
    block = lax.broadcasted_iota(jnp.int32, (local, n_exp, rows), 1)
    rank = tables[1].astype(jnp.int32)
    codes = jnp.where(rank >= 0, rank + CAP * block, -1)
    mix = tables[0].reshape(local, n_exp * rows)
    code = codes.reshape(local, n_exp * rows)
    piece_codes = [codes[:, j] for j in range(n_exp)] if direct else [code]

    groups = 2 if local % 2 == 0 and (local // 2) % 8 == 0 else 1
    size = local // groups
    owns, recvs = [], []
    for g in range(groups):
        at = slice(g * size, (g + 1) * size)
        own, send = up_call([c[at] for c in piece_codes], pieces, w_gate, w_up, g * size, slots)
        owns.append(own)
        recvs.append([rotate(send, "tensor", j) for j in range(1, n_ten)])

    me = lax.axis_index("dp").astype(jnp.int32).reshape(1)
    acc = None
    if groups == 1:
        acc = jnp.zeros((n_dp, n_exp * rows, w_down.shape[2] // n_dp), jnp.float32)
    for g in range(groups):
        at = slice(g * size, (g + 1) * size)
        acc = down_call(
            code[at], mix[at], owns[g], recvs[g], w_down, acc, g * size, slots, n_dp, me
        )

    part = acc[0]
    for k in range(1, n_dp):
        part = part + rotate(acc[k], "dp", k).astype(jnp.float32)
    if direct:
        mine = part[:rows]
        for j in range(1, n_exp):
            back = part[j * rows : (j + 1) * rows].astype(jnp.bfloat16)
            mine = mine + rotate(back, "expert", -j).astype(jnp.float32)
    else:
        mine = lax.psum_scatter(part, "expert", scatter_dimension=0, tiled=True)
    return lax.all_gather(mine.astype(jnp.bfloat16), "dp", axis=1, tiled=True)


def solution(mesh):
    in_specs = (
        P("expert", "tensor"),
        P("expert", None),
        P("expert", None),
        P("expert", "tensor", "dp"),
        P("expert", "tensor", "dp"),
        P("expert", "dp", "tensor"),
    )
    out_specs = P("expert", "tensor")
    return jax.shard_map(
        per_device, mesh=mesh, in_specs=in_specs, out_specs=out_specs, check_vma=False
    )
```

time: 220 us -> 96.9 us (0.44)
  blocking collectives: 68.6 us -> 5.53 us
  waiting for transfers between devices: 76.8 us -> 26.7 us
  Pallas kernels: 0 us -> 41.2 us
  matrix products: 38.1 us -> 0.19 us
  starting transfers between devices: 4.8 us -> 18.9 us
  between operations: 13.2 us -> 0.11 us
  local copies, waits for them, and re-layouts: 15.5 us -> 3.57 us
    reduce_scatter x3 -> x0, waiting for transfers between devices: 54.2 us -> none  [the longest x1 41.4 us: per_device(): lax.psum_scatter(partial_value, 'dp', scatter_dimension=1, tiled=True)]
    all_to_all x1 -> x0, blocking collectives: 48.7 us -> none  [per_device(): lax.all_to_all(outbound, 'expert', split_axis=2, concat_axis=2, tiled=True)]
    pallas_call x0 -> x4, Pallas kernels: none -> 41.2 us  [the longest x2 26.7 us: up_call(): pl.pallas_call(functools.partial(up_kernel, len(pieces), slots), grid=(ex...]
    dot_general x5 -> x1, matrix products: 38.1 us -> 0.19 us  [per_device(): jnp.dot(named.astype(jnp.bfloat16), earlier.astype(jnp.bfloat16), preferr...]
    ppermute x0 -> x14, waiting for transfers between devices: none -> 26.7 us  [rotate(): return lax.ppermute(x, axis, [(i, (i + shift) % n) for i in range(n)])]
    all_to_all x1 -> x0, waiting for transfers between devices: 22.5 us -> none  [per_device(): lax.all_to_all(backward, 'expert', split_axis=2, concat_axis=2, tiled=True)]
    ppermute x0 -> x14, starting transfers between devices: none -> 18.9 us  [rotate(): return lax.ppermute(x, axis, [(i, (i + shift) % n) for i in range(n)])]
    psum x1 -> x0, blocking collectives: 14.7 us -> none  [per_device(): mixed = lax.psum(partial_mix, 'dp')]
  transfers between devices with their start and end apart: 4 -> 14, of which waited for: 3 -> 9; matrix products, arithmetic and copies ran while one was open for 6% -> 0% of each run, Pallas kernels for 0% -> 21%
where the time goes in v1:
time: 96.9 us; the launch traced here: 96.6 us
  Pallas kernels  41.2 us (43%)
  waiting for transfers between devices  26.7 us (28%)
  starting transfers between devices  18.9 us (20%)
  blocking collectives  5.53 us (6%)
  local copies, waits for them, and re-layouts  3.57 us (4%)
    ppermute x14, waiting for transfers between devices, rotate(): return lax.ppermute(x, axis, [(i, (i + shift) % n) for i in range(n)])  26.7 us
    pallas_call x2, Pallas kernels, up_call(): pl.pallas_call(functools.partial(up_kernel, len(pieces), slots), grid=(ex...  26.7 us
    ppermute x14, starting transfers between devices, rotate(): return lax.ppermute(x, axis, [(i, (i + shift) % n) for i in range(n)])  18.9 us
    pallas_call x2, Pallas kernels, down_call(): pl.pallas_call(functools.partial(down_kernel, len(recvs), n_out, slots, l...  14.5 us
    all_gather x1, blocking collectives, per_device(): return lax.all_gather(mine.astype(jnp.bfloat16), 'dp', axis=1, tiled=True)  5.53 us
    unnamed x7, local copies, waits for them, and re-layouts  3.11 us
  transfers between devices with their start and end apart: 14, of which 9 were waited for; matrix products, arithmetic and copies ran while one was open for 0% of the time, Pallas kernels for 21%

profile of v1, /device:TPU:0, one launch (start us, length us, event | category | flops | bytes accessed | tf_op | source)
XLA Modules:
  0.0 96.6 jit_solution(15469968918462108878)
XLA Ops:
  0.0 0.8 copy.28
  0.8 0.1 fusion.1
  0.9 0.2 fusion
  1.1 0.8 copy.29
  1.8 0.1 select_reduce_fusion
  2.0 0.1 copy.30
  2.1 5.1 %collective-permute-start.2 = (f32[2,64,24]{2,1,0:T(8,128)S(1)}, f32[2,64,24]{2,1,0:T(8,128)S(1)}, u32[]{:S(2)}, u32[]{:S(2)}) collective-permute-start(f32[2,64,24]{2,1,0:T(8,128)S(1)} %copy.30), channel_id=1, source_target_pairs={{0,6},{2,0},{4,2},{6,4},{1,7},{3,1},{5,3},{7,5},{8,14},{10,8},{12,... | collective-permute-start | bytes 36872 | tf_op jit(solution)/shard_map/ppermute | solution.py:17
  7.2 0.0 collective-permute-start.1
  7.2 1.0 %collective-permute-start = (f32[2,64,24]{2,1,0:T(8,128)S(1)}, f32[2,64,24]{2,1,0:T(8,128)S(1)}, u32[]{:S(2)}, u32[]{:S(2)}) collective-permute-start(f32[2,64,24]{2,1,0:T(8,128)S(1)} %copy.30), channel_id=1, source_target_pairs={{0,2},{2,4},{4,6},{6,0},{1,3},{3,5},{5,7},{7,1},{8,10},{10,12},{12... | collective-permute-start | bytes 36872 | tf_op jit(solution)/shard_map/ppermute | solution.py:17
  8.2 2.8 %collective-permute-start.5 = (bf16[24,3584]{1,0:T(8,128)(2,1)}, bf16[24,3584]{1,0:T(8,128)(2,1)S(1)}, u32[]{:S(2)}, u32[]{:S(2)}) collective-permute-start(bf16[24,3584]{1,0:T(8,128)(2,1)} %refs_4_.3), channel_id=1, source_target_pairs={{0,6},{2,0},{4,2},{6,4},{1,7},{3,1},{5,3},{7,5},{8,14},{10,8},{12,... | collective-permute-start | bytes 516104 | tf_op jit(solution)/shard_map/ppermute | solution.py:17
  11.0 1.1 %collective-permute-start.4 = (bf16[24,3584]{1,0:T(8,128)(2,1)}, bf16[24,3584]{1,0:T(8,128)(2,1)S(1)}, u32[]{:S(2)}, u32[]{:S(2)}) collective-permute-start(bf16[24,3584]{1,0:T(8,128)(2,1)} %refs_4_.3), channel_id=1, source_target_pairs={{0,4},{2,6},{4,0},{6,2},{1,5},{3,7},{5,1},{7,3},{8,12},{10,14},{12... | collective-permute-start | bytes 516104 | tf_op jit(solution)/shard_map/ppermute | solution.py:17
  12.1 0.0 collective-permute-done.2
  12.1 0.0 collective-permute-start.3
  12.1 1.8 %collective-permute-done.1 = f32[2,64,24]{2,1,0:T(8,128)S(1)} collective-permute-done((f32[2,64,24]{2,1,0:T(8,128)S(1)}, f32[2,64,24]{2,1,0:T(8,128)S(1)}, u32[]{:S(2)}, u32[]{:S(2)}) %collective-permute-start.1) | collective-permute-done | bytes 12320 | tf_op jit(solution)/shard_map/ppermute | solution.py:17
  14.0 0.0 collective-permute-done
  14.0 0.1 add_select_fusion
  14.1 0.1 slice.121.refs_2_
  14.2 0.1 slice.109.refs_2_
  14.2 0.1 slice.119.refs_1_
  14.3 0.1 slice.107.refs_1_
  14.4 2.8 %collective-permute-done.5.refs_7_ = bf16[24,3584]{1,0:T(8,128)(2,1)S(1)} collective-permute-done((bf16[24,3584]{1,0:T(8,128)(2,1)}, bf16[24,3584]{1,0:T(8,128)(2,1)S(1)}, u32[]{:S(2)}, u32[]{:S(2)}) %collective-permute-start.5) | collective-permute-done | bytes 172064 | tf_op jit(solution)/shard_map/ppermute | solution.py:17
  17.2 11.2 %collective-permute-done.4.refs_6_ = bf16[24,3584]{1,0:T(8,128)(2,1)S(1)} collective-permute-done((bf16[24,3584]{1,0:T(8,128)(2,1)}, bf16[24,3584]{1,0:T(8,128)(2,1)S(1)}, u32[]{:S(2)}, u32[]{:S(2)}) %collective-permute-start.4) | collective-permute-done | bytes 172064 | tf_op jit(solution)/shard_map/ppermute | solution.py:17
  28.4 0.0 collective-permute-done.3.refs_5_
  28.4 0.9 copy-done
  29.3 13.4 %gate_up.3 = (f32[128,512]{1,0:T(8,128)S(1)}, bf16[128,512]{1,0:T(8,128)(2,1)S(1)}) custom-call(s32[8,24]{1,0:T(8,128)S(1)} %get-tuple-element.31.refs_0_, s32[8,24]{1,0:T(8,128)S(1)} %get-tuple-element.30.refs_1_, s32[8,24]{1,0:T(8,128)S(1)} %get-tuple-element.29.refs_2_, s32[8,24]{1,0:T(8,128)S(1)} %get-tuple-element.28.refs_3_, ...), custom_call_target="tpu_custom_call" | custom-call | flops 1468006400 | bytes 29360128 | tf_op jit(solution)/shard_map/gate_up/pallas_call | solution.py:62
  42.7 1.5 %collective-permute-start.7 = (bf16[128,512]{1,0:T(8,128)(2,1)S(1)}, bf16[128,512]{1,0:T(8,128)(2,1)S(1)}, u32[]{:S(2)}, u32[]{:S(2)}) collective-permute-start(bf16[128,512]{1,0:T(8,128)(2,1)S(1)} %get-tuple-element.16), channel_id=1, source_target_pairs={{0,1},{1,0},{2,3},{3,2},{4,5},{5,4},{6,7},{7,6},{8,9},{9,8},{10,11... | collective-permute-start | bytes 393224 | tf_op jit(solution)/shard_map/ppermute | solution.py:17
  44.2 0.0 copy-done.1
  44.2 13.3 %gate_up.2 = (f32[128,512]{1,0:T(8,128)S(1)}, bf16[128,512]{1,0:T(8,128)(2,1)S(1)}) custom-call(s32[8,24]{1,0:T(8,128)S(1)} %get-tuple-element.35.refs_0_, s32[8,24]{1,0:T(8,128)S(1)} %get-tuple-element.34.refs_1_, s32[8,24]{1,0:T(8,128)S(1)} %get-tuple-element.33.refs_2_, s32[8,24]{1,0:T(8,128)S(1)} %get-tuple-element.32.refs_3_, ...), custom_call_target="tpu_custom_call" | custom-call | flops 1468006400 | bytes 29360128 | tf_op jit(solution)/shard_map/gate_up/pallas_call | solution.py:62
  57.5 0.6 collective-permute-start.6
  58.1 0.0 collective-permute-done.7.refs_4_
  58.1 7.2 %down_mix.2.refs_6_ = f32[4,96,896]{2,1,0:T(8,128)S(1)} custom-call(s32[1]{0:T(128)} %bitcast.refs_0_, s32[8,96]{1,0:T(8,128)S(1)} %slice.119.refs_1_, f32[8,96]{1,0:T(8,128)S(1)} %slice.121.refs_2_, f32[128,512]{1,0:T(8,128)S(1)} %get-tuple-element.15.refs_3_, bf16[128,512]{1,0:T(8,128)(2,1)S(1)} %collective-permute-done.7.refs_4_, ...), custom_call_target="tpu_custom_call" | custom-call | flops 1468006400 | bytes 14680064 | tf_op jit(solution)/shard_map/down_mix/pallas_call | solution.py:163
  65.3 0.0 collective-permute-done.6.refs_4_
  65.3 7.3 %down_mix.3 = (f32[96,896]{1,0:T(8,128)S(1)}, bf16[96,896]{1,0:T(8,128)(2,1)S(1)}, bf16[96,896]{1,0:T(8,128)(2,1)S(1)}, bf16[96,896]{1,0:T(8,128)(2,1)S(1)}) custom-call(s32[1]{0:T(128)} %bitcast.refs_0_, s32[8,96]{1,0:T(8,128)S(1)} %slice.107.refs_1_, f32[8,96]{1,0:T(8,128)S(1)} %slice.109.refs_2_, f32[128,512]{1,0:T(8,128)S(1)} %get-tuple-element.13.refs_3_, ...), custom_call_target="tpu_custom_call" | custom-call | flops 1468006400 | bytes 14680064 | tf_op jit(solution)/shard_map/down_mix/pallas_call | solution.py:163
  72.6 0.1 collective-permute-start.8
  72.6 1.6 %collective-permute-start.9 = (bf16[96,896]{1,0:T(8,128)(2,1)S(1)}, bf16[96,896]{1,0:T(8,128)(2,1)S(1)}, u32[]{:S(2)}, u32[]{:S(2)}) collective-permute-start(bf16[96,896]{1,0:T(8,128)(2,1)S(1)} %get-tuple-element.19), channel_id=1, source_target_pairs={{0,16},{8,24},{16,0},{24,8},{1,17},{9,25},{17,1},{25,9},{2,18},{10... | collective-permute-start | bytes 516104 | tf_op jit(solution)/shard_map/ppermute | solution.py:17
  74.2 1.4 %collective-permute-start.10 = (bf16[96,896]{1,0:T(8,128)(2,1)S(1)}, bf16[96,896]{1,0:T(8,128)(2,1)S(1)}, u32[]{:S(2)}, u32[]{:S(2)}) collective-permute-start(bf16[96,896]{1,0:T(8,128)(2,1)S(1)} %get-tuple-element.20), channel_id=1, source_target_pairs={{0,24},{8,0},{16,8},{24,16},{1,25},{9,1},{17,9},{25,17},{2,26},{10... | collective-permute-start | bytes 516104 | tf_op jit(solution)/shard_map/ppermute | solution.py:17
  75.6 3.0 %collective-permute-done.8 = bf16[96,896]{1,0:T(8,128)(2,1)S(1)} collective-permute-done((bf16[96,896]{1,0:T(8,128)(2,1)S(1)}, bf16[96,896]{1,0:T(8,128)(2,1)S(1)}, u32[]{:S(2)}, u32[]{:S(2)}) %collective-permute-start.8) | collective-permute-done | bytes 172064 | tf_op jit(solution)/shard_map/ppermute | solution.py:17
  78.6 1.3 %collective-permute-done.9 = bf16[96,896]{1,0:T(8,128)(2,1)S(1)} collective-permute-done((bf16[96,896]{1,0:T(8,128)(2,1)S(1)}, bf16[96,896]{1,0:T(8,128)(2,1)S(1)}, u32[]{:S(2)}, u32[]{:S(2)}) %collective-permute-start.9) | collective-permute-done | bytes 172064 | tf_op jit(solution)/shard_map/ppermute | solution.py:17
  80.0 2.1 %collective-permute-done.10 = bf16[96,896]{1,0:T(8,128)(2,1)S(1)} collective-permute-done((bf16[96,896]{1,0:T(8,128)(2,1)S(1)}, bf16[96,896]{1,0:T(8,128)(2,1)S(1)}, u32[]{:S(2)}, u32[]{:S(2)}) %collective-permute-start.10) | collective-permute-done | bytes 172064 | tf_op jit(solution)/shard_map/ppermute | solution.py:17
  82.0 0.1 fusion.9
  82.1 0.1 collective-permute-start.11
  82.2 2.0 %collective-permute-start.13 = (bf16[24,896]{1,0:T(8,128)(2,1)S(1)}, bf16[24,896]{1,0:T(8,128)(2,1)S(1)}, u32[]{:S(2)}, u32[]{:S(2)}) collective-permute-start(bf16[24,896]{1,0:T(8,128)(2,1)S(1)} %get-tuple-element.24), channel_id=1, source_target_pairs={{0,2},{2,4},{4,6},{6,0},{1,3},{3,5},{5,7},{7,1},{8,10},{10,12},{12... | collective-permute-start | bytes 129032 | tf_op jit(solution)/shard_map/ppermute | solution.py:17
  84.2 1.7 %collective-permute-start.12 = (bf16[24,896]{1,0:T(8,128)(2,1)S(1)}, bf16[24,896]{1,0:T(8,128)(2,1)S(1)}, u32[]{:S(2)}, u32[]{:S(2)}) collective-permute-start(bf16[24,896]{1,0:T(8,128)(2,1)S(1)} %get-tuple-element.25), channel_id=1, source_target_pairs={{0,4},{2,6},{4,0},{6,2},{1,5},{3,7},{5,1},{7,3},{8,12},{10,14},{12... | collective-permute-start | bytes 129032 | tf_op jit(solution)/shard_map/ppermute | solution.py:17
  85.9 0.6 collective-permute-done.11
  86.5 2.3 %collective-permute-done.13 = bf16[24,896]{1,0:T(8,128)(2,1)S(1)} collective-permute-done((bf16[24,896]{1,0:T(8,128)(2,1)S(1)}, bf16[24,896]{1,0:T(8,128)(2,1)S(1)}, u32[]{:S(2)}, u32[]{:S(2)}) %collective-permute-start.13) | collective-permute-done | bytes 43040 | tf_op jit(solution)/shard_map/ppermute | solution.py:17
  88.8 1.6 %collective-permute-done.12 = bf16[24,896]{1,0:T(8,128)(2,1)S(1)} collective-permute-done((bf16[24,896]{1,0:T(8,128)(2,1)S(1)}, bf16[24,896]{1,0:T(8,128)(2,1)S(1)}, u32[]{:S(2)}, u32[]{:S(2)}) %collective-permute-start.12) | collective-permute-done | bytes 43040 | tf_op jit(solution)/shard_map/ppermute | solution.py:17
  90.4 5.5 %all_gather.3 = bf16[24,3584]{1,0:T(8,128)(2,1)S(1)} all-gather(bf16[24,896]{1,0:T(8,128)(2,1)S(1)} %fusion.4), channel_id=1, replica_groups=mesh['dp'=4,'expert'=4,'tensor'=2] {'dp'}, dimensions={1}, use_global_device_ids=true | all-gather | bytes 215040 | tf_op jit(solution)/shard_map/all_gather | solution.py:253
  96.0 0.7 copy.39
  (14 shorter events, 0.1 us)
Async XLA Ops:
  2.1 10.1 %collective-permute-start.2 = (f32[2,64,24]{2,1,0:T(8,128)S(1)}, f32[2,64,24]{2,1,0:T(8,128)S(1)}, u32[]{:S(2)}, u32[]{:S(2)}) collective-permute-start(f32[2,64,24]{2,1,0:T(8,128)S(1)} %copy.30), channel_id=1, source_target_pairs={{0,6},{2,0},{4,2},{6,4},{1,7},{3,1},{5,3},{7,5},{8,14},{10,8},{12,... | collective-permute-start | bytes 36872 | tf_op jit(solution)/shard_map/ppermute | solution.py:17
  7.2 6.8 %collective-permute-start.1 = (f32[2,64,24]{2,1,0:T(8,128)S(1)}, f32[2,64,24]{2,1,0:T(8,128)S(1)}, u32[]{:S(2)}, u32[]{:S(2)}) collective-permute-start(f32[2,64,24]{2,1,0:T(8,128)S(1)} %copy.30), channel_id=1, source_target_pairs={{0,4},{2,6},{4,0},{6,2},{1,5},{3,7},{5,1},{7,3},{8,12},{10,14},{12... | collective-permute-start | bytes 36872 | tf_op jit(solution)/shard_map/ppermute | solution.py:17
  7.2 6.8 %collective-permute-start = (f32[2,64,24]{2,1,0:T(8,128)S(1)}, f32[2,64,24]{2,1,0:T(8,128)S(1)}, u32[]{:S(2)}, u32[]{:S(2)}) collective-permute-start(f32[2,64,24]{2,1,0:T(8,128)S(1)} %copy.30), channel_id=1, source_target_pairs={{0,2},{2,4},{4,6},{6,0},{1,3},{3,5},{5,7},{7,1},{8,10},{10,12},{12... | collective-permute-start | bytes 36872 | tf_op jit(solution)/shard_map/ppermute | solution.py:17
  8.2 9.0 %collective-permute-start.5 = (bf16[24,3584]{1,0:T(8,128)(2,1)}, bf16[24,3584]{1,0:T(8,128)(2,1)S(1)}, u32[]{:S(2)}, u32[]{:S(2)}) collective-permute-start(bf16[24,3584]{1,0:T(8,128)(2,1)} %refs_4_.3), channel_id=1, source_target_pairs={{0,6},{2,0},{4,2},{6,4},{1,7},{3,1},{5,3},{7,5},{8,14},{10,8},{12,... | collective-permute-start | bytes 516104 | tf_op jit(solution)/shard_map/ppermute | solution.py:17
  11.0 17.4 %collective-permute-start.4 = (bf16[24,3584]{1,0:T(8,128)(2,1)}, bf16[24,3584]{1,0:T(8,128)(2,1)S(1)}, u32[]{:S(2)}, u32[]{:S(2)}) collective-permute-start(bf16[24,3584]{1,0:T(8,128)(2,1)} %refs_4_.3), channel_id=1, source_target_pairs={{0,4},{2,6},{4,0},{6,2},{1,5},{3,7},{5,1},{7,3},{8,12},{10,14},{12... | collective-permute-start | bytes 516104 | tf_op jit(solution)/shard_map/ppermute | solution.py:17
  12.1 16.3 %collective-permute-start.3 = (bf16[24,3584]{1,0:T(8,128)(2,1)}, bf16[24,3584]{1,0:T(8,128)(2,1)S(1)}, u32[]{:S(2)}, u32[]{:S(2)}) collective-permute-start(bf16[24,3584]{1,0:T(8,128)(2,1)} %refs_4_.3), channel_id=1, source_target_pairs={{0,2},{2,4},{4,6},{6,0},{1,3},{3,5},{5,7},{7,1},{8,10},{10,12},{12... | collective-permute-start | bytes 516104 | tf_op jit(solution)/shard_map/ppermute | solution.py:17
  28.4 0.9 copy-start
  29.3 14.9 %copy-start.1 = (bf16[24,3584]{1,0:T(8,128)(2,1)S(1)}, bf16[24,3584]{1,0:T(8,128)(2,1)}, u32[]{:S(2)}) copy-start(bf16[24,3584]{1,0:T(8,128)(2,1)} %refs_4_.3) | copy-start | bytes 516100
  42.7 15.4 %collective-permute-start.7 = (bf16[128,512]{1,0:T(8,128)(2,1)S(1)}, bf16[128,512]{1,0:T(8,128)(2,1)S(1)}, u32[]{:S(2)}, u32[]{:S(2)}) collective-permute-start(bf16[128,512]{1,0:T(8,128)(2,1)S(1)} %get-tuple-element.16), channel_id=1, source_target_pairs={{0,1},{1,0},{2,3},{3,2},{4,5},{5,4},{6,7},{7,6},{8,9},{9,8},{10,11... | collective-permute-start | bytes 393224 | tf_op jit(solution)/shard_map/ppermute | solution.py:17
  57.5 7.8 %collective-permute-start.6 = (bf16[128,512]{1,0:T(8,128)(2,1)S(1)}, bf16[128,512]{1,0:T(8,128)(2,1)S(1)}, u32[]{:S(2)}, u32[]{:S(2)}) collective-permute-start(bf16[128,512]{1,0:T(8,128)(2,1)S(1)} %get-tuple-element.14), channel_id=1, source_target_pairs={{0,1},{1,0},{2,3},{3,2},{4,5},{5,4},{6,7},{7,6},{8,9},{9,8},{10,11... | collective-permute-start | bytes 393224 | tf_op jit(solution)/shard_map/ppermute | solution.py:17
  72.6 6.1 %collective-permute-start.8 = (bf16[96,896]{1,0:T(8,128)(2,1)S(1)}, bf16[96,896]{1,0:T(8,128)(2,1)S(1)}, u32[]{:S(2)}, u32[]{:S(2)}) collective-permute-start(bf16[96,896]{1,0:T(8,128)(2,1)S(1)} %get-tuple-element.18), channel_id=1, source_target_pairs={{0,8},{8,16},{16,24},{24,0},{1,9},{9,17},{17,25},{25,1},{2,10},{10... | collective-permute-start | bytes 516104 | tf_op jit(solution)/shard_map/ppermute | solution.py:17
  72.6 7.3 %collective-permute-start.9 = (bf16[96,896]{1,0:T(8,128)(2,1)S(1)}, bf16[96,896]{1,0:T(8,128)(2,1)S(1)}, u32[]{:S(2)}, u32[]{:S(2)}) collective-permute-start(bf16[96,896]{1,0:T(8,128)(2,1)S(1)} %get-tuple-element.19), channel_id=1, source_target_pairs={{0,16},{8,24},{16,0},{24,8},{1,17},{9,25},{17,1},{25,9},{2,18},{10... | collective-permute-start | bytes 516104 | tf_op jit(solution)/shard_map/ppermute | solution.py:17
  74.2 7.8 %collective-permute-start.10 = (bf16[96,896]{1,0:T(8,128)(2,1)S(1)}, bf16[96,896]{1,0:T(8,128)(2,1)S(1)}, u32[]{:S(2)}, u32[]{:S(2)}) collective-permute-start(bf16[96,896]{1,0:T(8,128)(2,1)S(1)} %get-tuple-element.20), channel_id=1, source_target_pairs={{0,24},{8,0},{16,8},{24,16},{1,25},{9,1},{17,9},{25,17},{2,26},{10... | collective-permute-start | bytes 516104 | tf_op jit(solution)/shard_map/ppermute | solution.py:17
  82.1 4.4 %collective-permute-start.11 = (bf16[24,896]{1,0:T(8,128)(2,1)S(1)}, bf16[24,896]{1,0:T(8,128)(2,1)S(1)}, u32[]{:S(2)}, u32[]{:S(2)}) collective-permute-start(bf16[24,896]{1,0:T(8,128)(2,1)S(1)} %get-tuple-element.23), channel_id=1, source_target_pairs={{0,6},{2,0},{4,2},{6,4},{1,7},{3,1},{5,3},{7,5},{8,14},{10,8},{12,... | collective-permute-start | bytes 129032 | tf_op jit(solution)/shard_map/ppermute | solution.py:17
  82.2 6.6 %collective-permute-start.13 = (bf16[24,896]{1,0:T(8,128)(2,1)S(1)}, bf16[24,896]{1,0:T(8,128)(2,1)S(1)}, u32[]{:S(2)}, u32[]{:S(2)}) collective-permute-start(bf16[24,896]{1,0:T(8,128)(2,1)S(1)} %get-tuple-element.24), channel_id=1, source_target_pairs={{0,2},{2,4},{4,6},{6,0},{1,3},{3,5},{5,7},{7,1},{8,10},{10,12},{12... | collective-permute-start | bytes 129032 | tf_op jit(solution)/shard_map/ppermute | solution.py:17
  84.2 6.2 %collective-permute-start.12 = (bf16[24,896]{1,0:T(8,128)(2,1)S(1)}, bf16[24,896]{1,0:T(8,128)(2,1)S(1)}, u32[]{:S(2)}, u32[]{:S(2)}) collective-permute-start(bf16[24,896]{1,0:T(8,128)(2,1)S(1)} %get-tuple-element.25), channel_id=1, source_target_pairs={{0,4},{2,6},{4,0},{6,2},{1,5},{3,7},{5,1},{7,3},{8,12},{10,14},{12... | collective-permute-start | bytes 129032 | tf_op jit(solution)/shard_map/ppermute | solution.py:17

commit v2 on v1

--- a/solution.py
+++ b/solution.py
@@ -208,6 +208,8 @@
 
     if direct:
         pieces = [tokens] + [rotate(tokens, "expert", j) for j in range(1, n_exp)]
+        if n_exp > 1:
+            table, pieces[1] = lax.optimization_barrier((table, pieces[1]))
         tables = [table] + [rotate(table, "expert", j) for j in range(1, n_exp)]
         tables = jnp.stack(tables, axis=2)
     else:

time: 96.9 us -> 99.6 us (1.028)
  starting transfers between devices: 18.9 us -> 23 us
  waiting for transfers between devices: 26.7 us -> 25.3 us
    ppermute x14, starting transfers between devices: 18.9 us -> 23 us  [rotate(): return lax.ppermute(x, axis, [(i, (i + shift) % n) for i in range(n)])]
    ppermute x14, waiting for transfers between devices: 26.7 us -> 25.3 us  [rotate(): return lax.ppermute(x, axis, [(i, (i + shift) % n) for i in range(n)])]
  transfers between devices with their start and end apart: 14 -> 14, of which waited for: 9 -> 9; matrix products, arithmetic and copies ran while one was open for 0% -> 3% of each run, Pallas kernels for 21% -> 21%
where the time goes in v2:
time: 99.6 us; the launch traced here: 99.3 us
  Pallas kernels  41.1 us (41%)
  waiting for transfers between devices  25.3 us (25%)
  starting transfers between devices  23 us (23%)
  blocking collectives  5.53 us (6%)
  local copies, waits for them, and re-layouts  3.56 us (4%)
    pallas_call x2, Pallas kernels, up_call(): pl.pallas_call(functools.partial(up_kernel, len(pieces), slots), grid=(ex...  26.7 us
    ppermute x14, waiting for transfers between devices, rotate(): return lax.ppermute(x, axis, [(i, (i + shift) % n) for i in range(n)])  25.3 us
    ppermute x14, starting transfers between devices, rotate(): return lax.ppermute(x, axis, [(i, (i + shift) % n) for i in range(n)])  23 us
    pallas_call x2, Pallas kernels, down_call(): pl.pallas_call(functools.partial(down_kernel, len(recvs), n_out, slots, l...  14.5 us
    all_gather x1, blocking collectives, per_device(): return lax.all_gather(mine.astype(jnp.bfloat16), 'dp', axis=1, tiled=True)  5.53 us
    unnamed x7, local copies, waits for them, and re-layouts  3.11 us
  transfers between devices with their start and end apart: 14, of which 9 were waited for; matrix products, arithmetic and copies ran while one was open for 3% of the time, Pallas kernels for 21%

profile of v2, /device:TPU:0, one launch (start us, length us, event | category | flops | bytes accessed | tf_op | source)
XLA Modules:
  0.0 99.3 jit_solution(3964108328727733464)
XLA Ops:
  0.0 5.1 %collective-permute-start.5 = (bf16[24,3584]{1,0:T(8,128)(2,1)}, bf16[24,3584]{1,0:T(8,128)(2,1)S(1)}, u32[]{:S(2)}, u32[]{:S(2)}) collective-permute-start(bf16[24,3584]{1,0:T(8,128)(2,1)} %refs_4_.3), channel_id=1, source_target_pairs={{0,6},{2,0},{4,2},{6,4},{1,7},{3,1},{5,3},{7,5},{8,14},{10,8},{12,... | collective-permute-start | bytes 516104 | tf_op jit(solution)/shard_map/ppermute | solution.py:17
  5.1 0.0 collective-permute-start.4
  5.1 1.0 %collective-permute-start = (bf16[24,3584]{1,0:T(8,128)(2,1)}, bf16[24,3584]{1,0:T(8,128)(2,1)S(1)}, u32[]{:S(2)}, u32[]{:S(2)}) collective-permute-start(bf16[24,3584]{1,0:T(8,128)(2,1)} %refs_4_.3), channel_id=1, source_target_pairs={{0,2},{2,4},{4,6},{6,0},{1,3},{3,5},{5,7},{7,1},{8,10},{10,12},{12... | collective-permute-start | bytes 516104 | tf_op jit(solution)/shard_map/ppermute | solution.py:17
  6.1 0.8 copy.28
  6.9 0.1 fusion.1
  7.0 0.8 copy.29
  7.7 0.1 select_reduce_fusion
  7.9 0.2 fusion
  8.1 9.2 %collective-permute-done.refs_5_ = bf16[24,3584]{1,0:T(8,128)(2,1)S(1)} collective-permute-done((bf16[24,3584]{1,0:T(8,128)(2,1)}, bf16[24,3584]{1,0:T(8,128)(2,1)S(1)}, u32[]{:S(2)}, u32[]{:S(2)}) %collective-permute-start) | collective-permute-done | bytes 172064 | tf_op jit(solution)/shard_map/ppermute | solution.py:17
  17.3 0.1 copy.30
  17.4 0.7 collective-permute-start.3
  18.1 6.2 %collective-permute-start.2 = (f32[2,64,24]{2,1,0:T(8,128)S(1)}, f32[2,64,24]{2,1,0:T(8,128)S(1)}, u32[]{:S(2)}, u32[]{:S(2)}) collective-permute-start(f32[2,64,24]{2,1,0:T(8,128)S(1)} %copy.30), channel_id=1, source_target_pairs={{0,4},{2,6},{4,0},{6,2},{1,5},{3,7},{5,1},{7,3},{8,12},{10,14},{12... | collective-permute-start | bytes 36872 | tf_op jit(solution)/shard_map/ppermute | solution.py:17
  24.3 1.9 %collective-permute-start.1 = (f32[2,64,24]{2,1,0:T(8,128)S(1)}, f32[2,64,24]{2,1,0:T(8,128)S(1)}, u32[]{:S(2)}, u32[]{:S(2)}) collective-permute-start(f32[2,64,24]{2,1,0:T(8,128)S(1)} %copy.30), channel_id=1, source_target_pairs={{0,2},{2,4},{4,6},{6,0},{1,3},{3,5},{5,7},{7,1},{8,10},{10,12},{12... | collective-permute-start | bytes 36872 | tf_op jit(solution)/shard_map/ppermute | solution.py:17
  26.2 0.0 collective-permute-done.3
  26.2 1.8 %collective-permute-done.2 = f32[2,64,24]{2,1,0:T(8,128)S(1)} collective-permute-done((f32[2,64,24]{2,1,0:T(8,128)S(1)}, f32[2,64,24]{2,1,0:T(8,128)S(1)}, u32[]{:S(2)}, u32[]{:S(2)}) %collective-permute-start.2) | collective-permute-done | bytes 12320 | tf_op jit(solution)/shard_map/ppermute | solution.py:17
  28.0 2.3 %collective-permute-done.1 = f32[2,64,24]{2,1,0:T(8,128)S(1)} collective-permute-done((f32[2,64,24]{2,1,0:T(8,128)S(1)}, f32[2,64,24]{2,1,0:T(8,128)S(1)}, u32[]{:S(2)}, u32[]{:S(2)}) %collective-permute-start.1) | collective-permute-done | bytes 12320 | tf_op jit(solution)/shard_map/ppermute | solution.py:17
  30.3 0.1 add_select_fusion
  30.4 0.1 slice.121.refs_2_
  30.5 0.1 slice.109.refs_2_
  30.6 0.1 slice.119.refs_1_
  30.7 0.1 slice.107.refs_1_
  30.8 0.0 collective-permute-done.5.refs_7_
  30.8 0.0 collective-permute-done.4.refs_6_
  30.8 0.0 copy-start
  30.8 0.9 copy-done
  31.7 13.4 %gate_up.3 = (f32[128,512]{1,0:T(8,128)S(1)}, bf16[128,512]{1,0:T(8,128)(2,1)S(1)}) custom-call(s32[8,24]{1,0:T(8,128)S(1)} %get-tuple-element.35.refs_0_, s32[8,24]{1,0:T(8,128)S(1)} %get-tuple-element.34.refs_1_, s32[8,24]{1,0:T(8,128)S(1)} %get-tuple-element.33.refs_2_, s32[8,24]{1,0:T(8,128)S(1)} %get-tuple-element.32.refs_3_, ...), custom_call_target="tpu_custom_call" | custom-call | flops 1468006400 | bytes 29360128 | tf_op jit(solution)/shard_map/gate_up/pallas_call | solution.py:62
  45.1 1.5 %collective-permute-start.7 = (bf16[128,512]{1,0:T(8,128)(2,1)S(1)}, bf16[128,512]{1,0:T(8,128)(2,1)S(1)}, u32[]{:S(2)}, u32[]{:S(2)}) collective-permute-start(bf16[128,512]{1,0:T(8,128)(2,1)S(1)} %get-tuple-element.20), channel_id=1, source_target_pairs={{0,1},{1,0},{2,3},{3,2},{4,5},{5,4},{6,7},{7,6},{8,9},{9,8},{10,11... | collective-permute-start | bytes 393224 | tf_op jit(solution)/shard_map/ppermute | solution.py:17
  46.6 13.3 %gate_up.2 = (f32[128,512]{1,0:T(8,128)S(1)}, bf16[128,512]{1,0:T(8,128)(2,1)S(1)}) custom-call(s32[8,24]{1,0:T(8,128)S(1)} %get-tuple-element.39.refs_0_, s32[8,24]{1,0:T(8,128)S(1)} %get-tuple-element.38.refs_1_, s32[8,24]{1,0:T(8,128)S(1)} %get-tuple-element.37.refs_2_, s32[8,24]{1,0:T(8,128)S(1)} %get-tuple-element.36.refs_3_, ...), custom_call_target="tpu_custom_call" | custom-call | flops 1468006400 | bytes 29360128 | tf_op jit(solution)/shard_map/gate_up/pallas_call | solution.py:62
  59.9 0.5 collective-permute-start.6
  60.5 0.0 collective-permute-done.7.refs_4_
  60.5 7.2 %down_mix.2.refs_6_ = f32[4,96,896]{2,1,0:T(8,128)S(1)} custom-call(s32[1]{0:T(128)} %bitcast.refs_0_, s32[8,96]{1,0:T(8,128)S(1)} %slice.119.refs_1_, f32[8,96]{1,0:T(8,128)S(1)} %slice.121.refs_2_, f32[128,512]{1,0:T(8,128)S(1)} %get-tuple-element.19.refs_3_, bf16[128,512]{1,0:T(8,128)(2,1)S(1)} %collective-permute-done.7.refs_4_, ...), custom_call_target="tpu_custom_call" | custom-call | flops 1468006400 | bytes 14680064 | tf_op jit(solution)/shard_map/down_mix/pallas_call | solution.py:163
  67.7 0.0 collective-permute-done.6.refs_4_
  67.7 7.3 %down_mix.3 = (f32[96,896]{1,0:T(8,128)S(1)}, bf16[96,896]{1,0:T(8,128)(2,1)S(1)}, bf16[96,896]{1,0:T(8,128)(2,1)S(1)}, bf16[96,896]{1,0:T(8,128)(2,1)S(1)}) custom-call(s32[1]{0:T(128)} %bitcast.refs_0_, s32[8,96]{1,0:T(8,128)S(1)} %slice.107.refs_1_, f32[8,96]{1,0:T(8,128)S(1)} %slice.109.refs_2_, f32[128,512]{1,0:T(8,128)S(1)} %get-tuple-element.17.refs_3_, ...), custom_call_target="tpu_custom_call" | custom-call | flops 1468006400 | bytes 14680064 | tf_op jit(solution)/shard_map/down_mix/pallas_call | solution.py:163
  75.0 0.1 collective-permute-start.8
  75.0 1.6 %collective-permute-start.9 = (bf16[96,896]{1,0:T(8,128)(2,1)S(1)}, bf16[96,896]{1,0:T(8,128)(2,1)S(1)}, u32[]{:S(2)}, u32[]{:S(2)}) collective-permute-start(bf16[96,896]{1,0:T(8,128)(2,1)S(1)} %get-tuple-element.23), channel_id=1, source_target_pairs={{0,16},{8,24},{16,0},{24,8},{1,17},{9,25},{17,1},{25,9},{2,18},{10... | collective-permute-start | bytes 516104 | tf_op jit(solution)/shard_map/ppermute | solution.py:17
  76.6 1.4 %collective-permute-start.10 = (bf16[96,896]{1,0:T(8,128)(2,1)S(1)}, bf16[96,896]{1,0:T(8,128)(2,1)S(1)}, u32[]{:S(2)}, u32[]{:S(2)}) collective-permute-start(bf16[96,896]{1,0:T(8,128)(2,1)S(1)} %get-tuple-element.24), channel_id=1, source_target_pairs={{0,24},{8,0},{16,8},{24,16},{1,25},{9,1},{17,9},{25,17},{2,26},{10... | collective-permute-start | bytes 516104 | tf_op jit(solution)/shard_map/ppermute | solution.py:17
  78.0 3.0 %collective-permute-done.8 = bf16[96,896]{1,0:T(8,128)(2,1)S(1)} collective-permute-done((bf16[96,896]{1,0:T(8,128)(2,1)S(1)}, bf16[96,896]{1,0:T(8,128)(2,1)S(1)}, u32[]{:S(2)}, u32[]{:S(2)}) %collective-permute-start.8) | collective-permute-done | bytes 172064 | tf_op jit(solution)/shard_map/ppermute | solution.py:17
  81.0 1.3 %collective-permute-done.9 = bf16[96,896]{1,0:T(8,128)(2,1)S(1)} collective-permute-done((bf16[96,896]{1,0:T(8,128)(2,1)S(1)}, bf16[96,896]{1,0:T(8,128)(2,1)S(1)}, u32[]{:S(2)}, u32[]{:S(2)}) %collective-permute-start.9) | collective-permute-done | bytes 172064 | tf_op jit(solution)/shard_map/ppermute | solution.py:17
  82.3 2.1 %collective-permute-done.10 = bf16[96,896]{1,0:T(8,128)(2,1)S(1)} collective-permute-done((bf16[96,896]{1,0:T(8,128)(2,1)S(1)}, bf16[96,896]{1,0:T(8,128)(2,1)S(1)}, u32[]{:S(2)}, u32[]{:S(2)}) %collective-permute-start.10) | collective-permute-done | bytes 172064 | tf_op jit(solution)/shard_map/ppermute | solution.py:17
  84.4 0.1 fusion.9
  84.5 1.2 %collective-permute-start.11 = (bf16[24,896]{1,0:T(8,128)(2,1)S(1)}, bf16[24,896]{1,0:T(8,128)(2,1)S(1)}, u32[]{:S(2)}, u32[]{:S(2)}) collective-permute-start(bf16[24,896]{1,0:T(8,128)(2,1)S(1)} %get-tuple-element.27), channel_id=1, source_target_pairs={{0,6},{2,0},{4,2},{6,4},{1,7},{3,1},{5,3},{7,5},{8,14},{10,8},{12,... | collective-permute-start | bytes 129032 | tf_op jit(solution)/shard_map/ppermute | solution.py:17
  85.7 0.9 collective-permute-start.13
  86.6 0.9 collective-permute-start.12
  87.5 1.3 %collective-permute-done.11 = bf16[24,896]{1,0:T(8,128)(2,1)S(1)} collective-permute-done((bf16[24,896]{1,0:T(8,128)(2,1)S(1)}, bf16[24,896]{1,0:T(8,128)(2,1)S(1)}, u32[]{:S(2)}, u32[]{:S(2)}) %collective-permute-start.11) | collective-permute-done | bytes 43040 | tf_op jit(solution)/shard_map/ppermute | solution.py:17
  88.9 3.2 %collective-permute-done.13 = bf16[24,896]{1,0:T(8,128)(2,1)S(1)} collective-permute-done((bf16[24,896]{1,0:T(8,128)(2,1)S(1)}, bf16[24,896]{1,0:T(8,128)(2,1)S(1)}, u32[]{:S(2)}, u32[]{:S(2)}) %collective-permute-start.13) | collective-permute-done | bytes 43040 | tf_op jit(solution)/shard_map/ppermute | solution.py:17
  92.1 1.0 %collective-permute-done.12 = bf16[24,896]{1,0:T(8,128)(2,1)S(1)} collective-permute-done((bf16[24,896]{1,0:T(8,128)(2,1)S(1)}, bf16[24,896]{1,0:T(8,128)(2,1)S(1)}, u32[]{:S(2)}, u32[]{:S(2)}) %collective-permute-start.12) | collective-permute-done | bytes 43040 | tf_op jit(solution)/shard_map/ppermute | solution.py:17
  93.1 5.5 %all_gather.3 = bf16[24,3584]{1,0:T(8,128)(2,1)S(1)} all-gather(bf16[24,896]{1,0:T(8,128)(2,1)S(1)} %fusion.4), channel_id=1, replica_groups=mesh['dp'=4,'expert'=4,'tensor'=2] {'dp'}, dimensions={1}, use_global_device_ids=true | all-gather | bytes 215040 | tf_op jit(solution)/shard_map/all_gather | solution.py:255
  98.6 0.7 copy.39
  (14 shorter events, 0.1 us)
Async XLA Ops:
  0.0 30.8 %collective-permute-start.5 = (bf16[24,3584]{1,0:T(8,128)(2,1)}, bf16[24,3584]{1,0:T(8,128)(2,1)S(1)}, u32[]{:S(2)}, u32[]{:S(2)}) collective-permute-start(bf16[24,3584]{1,0:T(8,128)(2,1)} %refs_4_.3), channel_id=1, source_target_pairs={{0,6},{2,0},{4,2},{6,4},{1,7},{3,1},{5,3},{7,5},{8,14},{10,8},{12,... | collective-permute-start | bytes 516104 | tf_op jit(solution)/shard_map/ppermute | solution.py:17
  5.1 25.7 %collective-permute-start.4 = (bf16[24,3584]{1,0:T(8,128)(2,1)}, bf16[24,3584]{1,0:T(8,128)(2,1)S(1)}, u32[]{:S(2)}, u32[]{:S(2)}) collective-permute-start(bf16[24,3584]{1,0:T(8,128)(2,1)} %refs_4_.3), channel_id=1, source_target_pairs={{0,4},{2,6},{4,0},{6,2},{1,5},{3,7},{5,1},{7,3},{8,12},{10,14},{12... | collective-permute-start | bytes 516104 | tf_op jit(solution)/shard_map/ppermute | solution.py:17
  5.1 12.2 %collective-permute-start = (bf16[24,3584]{1,0:T(8,128)(2,1)}, bf16[24,3584]{1,0:T(8,128)(2,1)S(1)}, u32[]{:S(2)}, u32[]{:S(2)}) collective-permute-start(bf16[24,3584]{1,0:T(8,128)(2,1)} %refs_4_.3), channel_id=1, source_target_pairs={{0,2},{2,4},{4,6},{6,0},{1,3},{3,5},{5,7},{7,1},{8,10},{10,12},{12... | collective-permute-start | bytes 516104 | tf_op jit(solution)/shard_map/ppermute | solution.py:17
  17.4 8.8 %collective-permute-start.3 = (f32[2,64,24]{2,1,0:T(8,128)S(1)}, f32[2,64,24]{2,1,0:T(8,128)S(1)}, u32[]{:S(2)}, u32[]{:S(2)}) collective-permute-start(f32[2,64,24]{2,1,0:T(8,128)S(1)} %copy.30), channel_id=1, source_target_pairs={{0,6},{2,0},{4,2},{6,4},{1,7},{3,1},{5,3},{7,5},{8,14},{10,8},{12,... | collective-permute-start | bytes 36872 | tf_op jit(solution)/shard_map/ppermute | solution.py:17
  18.1 9.9 %collective-permute-start.2 = (f32[2,64,24]{2,1,0:T(8,128)S(1)}, f32[2,64,24]{2,1,0:T(8,128)S(1)}, u32[]{:S(2)}, u32[]{:S(2)}) collective-permute-start(f32[2,64,24]{2,1,0:T(8,128)S(1)} %copy.30), channel_id=1, source_target_pairs={{0,4},{2,6},{4,0},{6,2},{1,5},{3,7},{5,1},{7,3},{8,12},{10,14},{12... | collective-permute-start | bytes 36872 | tf_op jit(solution)/shard_map/ppermute | solution.py:17
  24.3 6.1 %collective-permute-start.1 = (f32[2,64,24]{2,1,0:T(8,128)S(1)}, f32[2,64,24]{2,1,0:T(8,128)S(1)}, u32[]{:S(2)}, u32[]{:S(2)}) collective-permute-start(f32[2,64,24]{2,1,0:T(8,128)S(1)} %copy.30), channel_id=1, source_target_pairs={{0,2},{2,4},{4,6},{6,0},{1,3},{3,5},{5,7},{7,1},{8,10},{10,12},{12... | collective-permute-start | bytes 36872 | tf_op jit(solution)/shard_map/ppermute | solution.py:17
  30.8 0.9 copy-start
  31.7 14.9 %copy-start.1 = (bf16[24,3584]{1,0:T(8,128)(2,1)S(1)}, bf16[24,3584]{1,0:T(8,128)(2,1)}, u32[]{:S(2)}) copy-start(bf16[24,3584]{1,0:T(8,128)(2,1)} %refs_4_.3) | copy-start | bytes 516100
  45.1 15.4 %collective-permute-start.7 = (bf16[128,512]{1,0:T(8,128)(2,1)S(1)}, bf16[128,512]{1,0:T(8,128)(2,1)S(1)}, u32[]{:S(2)}, u32[]{:S(2)}) collective-permute-start(bf16[128,512]{1,0:T(8,128)(2,1)S(1)} %get-tuple-element.20), channel_id=1, source_target_pairs={{0,1},{1,0},{2,3},{3,2},{4,5},{5,4},{6,7},{7,6},{8,9},{9,8},{10,11... | collective-permute-start | bytes 393224 | tf_op jit(solution)/shard_map/ppermute | solution.py:17
  59.9 7.7 %collective-permute-start.6 = (bf16[128,512]{1,0:T(8,128)(2,1)S(1)}, bf16[128,512]{1,0:T(8,128)(2,1)S(1)}, u32[]{:S(2)}, u32[]{:S(2)}) collective-permute-start(bf16[128,512]{1,0:T(8,128)(2,1)S(1)} %get-tuple-element.18), channel_id=1, source_target_pairs={{0,1},{1,0},{2,3},{3,2},{4,5},{5,4},{6,7},{7,6},{8,9},{9,8},{10,11... | collective-permute-start | bytes 393224 | tf_op jit(solution)/shard_map/ppermute | solution.py:17
  75.0 6.1 %collective-permute-start.8 = (bf16[96,896]{1,0:T(8,128)(2,1)S(1)}, bf16[96,896]{1,0:T(8,128)(2,1)S(1)}, u32[]{:S(2)}, u32[]{:S(2)}) collective-permute-start(bf16[96,896]{1,0:T(8,128)(2,1)S(1)} %get-tuple-element.22), channel_id=1, source_target_pairs={{0,8},{8,16},{16,24},{24,0},{1,9},{9,17},{17,25},{25,1},{2,10},{10... | collective-permute-start | bytes 516104 | tf_op jit(solution)/shard_map/ppermute | solution.py:17
  75.0 7.3 %collective-permute-start.9 = (bf16[96,896]{1,0:T(8,128)(2,1)S(1)}, bf16[96,896]{1,0:T(8,128)(2,1)S(1)}, u32[]{:S(2)}, u32[]{:S(2)}) collective-permute-start(bf16[96,896]{1,0:T(8,128)(2,1)S(1)} %get-tuple-element.23), channel_id=1, source_target_pairs={{0,16},{8,24},{16,0},{24,8},{1,17},{9,25},{17,1},{25,9},{2,18},{10... | collective-permute-start | bytes 516104 | tf_op jit(solution)/shard_map/ppermute | solution.py:17
  76.6 7.8 %collective-permute-start.10 = (bf16[96,896]{1,0:T(8,128)(2,1)S(1)}, bf16[96,896]{1,0:T(8,128)(2,1)S(1)}, u32[]{:S(2)}, u32[]{:S(2)}) collective-permute-start(bf16[96,896]{1,0:T(8,128)(2,1)S(1)} %get-tuple-element.24), channel_id=1, source_target_pairs={{0,24},{8,0},{16,8},{24,16},{1,25},{9,1},{17,9},{25,17},{2,26},{10... | collective-permute-start | bytes 516104 | tf_op jit(solution)/shard_map/ppermute | solution.py:17
  84.5 4.4 %collective-permute-start.11 = (bf16[24,896]{1,0:T(8,128)(2,1)S(1)}, bf16[24,896]{1,0:T(8,128)(2,1)S(1)}, u32[]{:S(2)}, u32[]{:S(2)}) collective-permute-start(bf16[24,896]{1,0:T(8,128)(2,1)S(1)} %get-tuple-element.27), channel_id=1, source_target_pairs={{0,6},{2,0},{4,2},{6,4},{1,7},{3,1},{5,3},{7,5},{8,14},{10,8},{12,... | collective-permute-start | bytes 129032 | tf_op jit(solution)/shard_map/ppermute | solution.py:17
  85.7 6.4 %collective-permute-start.13 = (bf16[24,896]{1,0:T(8,128)(2,1)S(1)}, bf16[24,896]{1,0:T(8,128)(2,1)S(1)}, u32[]{:S(2)}, u32[]{:S(2)}) collective-permute-start(bf16[24,896]{1,0:T(8,128)(2,1)S(1)} %get-tuple-element.28), channel_id=1, source_target_pairs={{0,2},{2,4},{4,6},{6,0},{1,3},{3,5},{5,7},{7,1},{8,10},{10,12},{12... | collective-permute-start | bytes 129032 | tf_op jit(solution)/shard_map/ppermute | solution.py:17
  86.6 6.5 %collective-permute-start.12 = (bf16[24,896]{1,0:T(8,128)(2,1)S(1)}, bf16[24,896]{1,0:T(8,128)(2,1)S(1)}, u32[]{:S(2)}, u32[]{:S(2)}) collective-permute-start(bf16[24,896]{1,0:T(8,128)(2,1)S(1)} %get-tuple-element.29), channel_id=1, source_target_pairs={{0,4},{2,6},{4,0},{6,2},{1,5},{3,7},{5,1},{7,3},{8,12},{10,14},{12... | collective-permute-start | bytes 129032 | tf_op jit(solution)/shard_map/ppermute | solution.py:17
